TPU v7x, 256 devices: a whole 4x4x8 slice. The times are simulated.
256 devices in a mesh: wide: 64 (over x, y_hi, z), narrow: 4 (over y_lo, core).
Axes of the slice: x: 4, y: 4 (y_hi: 2, y_lo: 2; y = y_hi * 2 + y_lo), z: 8, core: 2. Of those that a mesh axis runs over, the one named last changes fastest.
Arguments:
- tokens: bfloat16 [8192, 2048], P('wide'), may hold values from -6 to 6
- expert_ids: int32 [8192, 6], P('wide'), may hold values from 0 to 63, all different within a row; in each aligned block of 128 rows (0 to 127, 128 to 255, ...) at most 16 rows name the same one
- gate_weights: float32 [8192, 6], P('wide'), may hold values from 0.05 to 0.6
- shared_gate: bfloat16 [2048, 2816], P('wide', 'narrow'), may hold values from -0.125 to 0.125
- shared_up: bfloat16 [2048, 2816], P('wide', 'narrow'), may hold values from -0.125 to 0.125
- shared_down: bfloat16 [2816, 2048], P('narrow', 'wide'), may hold values from -0.109375 to 0.109375
- expert_gate: bfloat16 [64, 2048, 1408], P('wide', None, 'narrow'), may hold values from -0.125 to 0.125
- expert_up: bfloat16 [64, 2048, 1408], P('wide', None, 'narrow'), may hold values from -0.125 to 0.125
- expert_down: bfloat16 [64, 1408, 2048], P('wide', 'narrow'), may hold values from -0.15625 to 0.15625
Outputs:
- moe_out: bfloat16 [8192, 2048], P('wide', 'narrow')
Inputs may be any that keep to these rules, and one draw needn't show every extreme that they name: `expert_ids`: the 6 ids of a row differ. Among the 128 rows of one index of wide, no expert is named by more than 16 rows.
All inputs are finite; a program needn't handle non-finite values.
Results may differ from a plain program's by a relative error of at most 0.0075.
Values may be sent and summed in bfloat16 or wider, within the bound.
No kernel may reach another device: no remote copies, remote signals or barrier semaphores. Data moves between devices by JAX's collectives and lax.ppermute only.
A program may use at most 128 MiB of HBM per device.

v0:
```python
import jax
import jax.numpy as jnp
from jax import lax
from jax.sharding import PartitionSpec as P


def items_in_groups(array, axis, split_dim, concat_dim, work, item_dim, out_dim):
    items = jax.tree.leaves(array)[0].shape[item_dim]
    count = 2 if items % 2 == 0 else 1
    finished = []
    for k in range(count):
        group = jax.tree.map(
            lambda a: lax.slice_in_dim(
                a, k * (items // count), (k + 1) * (items // count), axis=item_dim
            ),
            array,
        )
        finished.append(
            work(
                lax.all_to_all(
                    group, axis, split_axis=split_dim, concat_axis=concat_dim, tiled=True
                )
            )
        )
    return jax.tree.map(lambda *parts: jnp.concatenate(parts, axis=out_dim), *finished)


def split_up(array, dim, length):
    lengths = array.shape
    blocks = array.reshape(*lengths[:dim], length, lengths[dim] // length, *lengths[dim + 1 :])
    return jnp.moveaxis(blocks, dim, 0)


def sum_at_owner(array, axis, dim):
    length = lax.axis_size(axis)
    blocks = lax.all_to_all(split_up(array, dim, length), axis, 0, 0, tiled=True)
    return jnp.sum(blocks.astype(jnp.float32), axis=0)


def sent_together(arrays, axis, dim, along):
    ends, at = ([], 0)
    for a in arrays[:-1]:
        at += a.shape[along]
        ends.append(at)
    both = jnp.concatenate(arrays, axis=along)
    return tuple(jnp.split(lax.all_gather(both, axis, axis=dim, tiled=True), ends, axis=along))


def expert_ffn(received, w_gate, w_up, w_down):
    senders, items, width = received.shape
    flat_rows = received.reshape(senders * items, width)
    gate_part = jnp.dot(flat_rows, w_gate, preferred_element_type=jnp.float32)
    up_part = jnp.dot(flat_rows, w_up, preferred_element_type=jnp.float32)
    hidden = (jax.nn.silu(gate_part) * up_part).astype(jnp.bfloat16)
    partial_value = jnp.dot(hidden, w_down, preferred_element_type=jnp.float32).astype(jnp.bfloat16)
    return partial_value.reshape(senders, items, w_down.shape[1])


def body(
    tokens,
    expert_ids,
    gate_weights,
    shared_gate,
    shared_up,
    shared_down,
    expert_gate,
    expert_up,
    expert_down,
):
    tok_count, width = tokens.shape
    top_count = expert_ids.shape[1]
    experts = lax.axis_size("wide") * expert_gate.shape[0]
    capacity = min(tok_count, 4 * tok_count * top_count // (3 * experts))
    w_gate = expert_gate[0]
    w_up = expert_up[0]
    w_down = expert_down[0]
    pairs = tok_count * top_count
    flat_ids = expert_ids.reshape(pairs)
    onehot = (flat_ids[:, None] == jnp.arange(experts, dtype=jnp.int32)[None, :]).astype(jnp.int32)
    before = jnp.cumsum(onehot, axis=0) - onehot
    slot_pos = jnp.sum(before * onehot, axis=1)
    target_slot = flat_ids * capacity + slot_pos
    source = (
        jnp.full((experts * capacity,), -1, jnp.int32)
        .at[target_slot]
        .set(jnp.arange(pairs, dtype=jnp.int32))
    )
    filled = source >= 0
    token_of = jnp.where(filled, source // top_count, 0)
    outgoing = jnp.where(filled[:, None], tokens[token_of], jnp.zeros((), jnp.bfloat16))
    outgoing = outgoing.reshape(experts, capacity, width)

    def run_expert(received):
        return expert_ffn(received, w_gate, w_up, w_down)

    partial_value = items_in_groups(outgoing, "wide", 0, 0, run_expert, 1, 1)
    expert_out = sum_at_owner(partial_value, "narrow", 2).astype(jnp.bfloat16)
    returned = lax.all_to_all(expert_out, "wide", split_axis=0, concat_axis=0, tiled=True)
    returned_rows = returned.reshape(experts * capacity, returned.shape[2])
    pair_rows = returned_rows[target_slot].astype(jnp.float32)
    weighted = gate_weights.reshape(pairs, 1) * pair_rows
    routed = jnp.sum(weighted.reshape(tok_count, top_count, returned.shape[2]), axis=1)
    blocks = sent_together((shared_gate, shared_up), "wide", 0, 1)
    gate_sum = jnp.dot(tokens, blocks[0], preferred_element_type=jnp.float32)
    up_sum = jnp.dot(tokens, blocks[1], preferred_element_type=jnp.float32)
    shared_hidden = (jax.nn.silu(gate_sum) * up_sum).astype(jnp.bfloat16)
    shared_terms = jnp.dot(
        shared_hidden,
        lax.all_gather(shared_down, "wide", axis=1, tiled=True),
        preferred_element_type=jnp.float32,
    )
    shared = sum_at_owner(shared_terms.astype(jnp.bfloat16), "narrow", 1)
    return (shared + routed).astype(jnp.bfloat16)


def solution(mesh):
    in_specs = (
        P("wide", None),
        P("wide", None),
        P("wide", None),
        P("wide", "narrow"),
        P("wide", "narrow"),
        P("narrow", "wide"),
        P("wide", None, "narrow"),
        P("wide", None, "narrow"),
        P("wide", "narrow", None),
    )
    out_specs = P("wide", "narrow")
    return jax.shard_map(body, mesh=mesh, in_specs=in_specs, out_specs=out_specs, check_vma=False)
```

profile of v0, /device:TPU:1, one launch (start us, length us, event | category | flops | bytes accessed | tf_op | source)
XLA Modules:
  0.0 334.1 jit_solution(4834467579335310039)
XLA Ops:
  6.5 1.7 pad_maximum_fusion.1
  10.3 1.8 reduce-window.6
  12.6 3.4 %scatter_custom_fusion = s32[1024]{0:T(1024)S(1)} fusion(s32[768]{0:T(1024)S(1)} %fusion.85, s32[768]{0:T(1024)S(1)} %iota.11, s32[]{:T(128)} %constant.16.clone.1), kind=kCustom, calls=%fused_computation.79 | custom fusion | bytes 4100 | tf_op jit(solution)/shard_map/scatter | solution.py:86
  16.1 6.1 %gather_fusion = bf16[1024,2048]{1,0:T(8,128)(2,1)} fusion(bf16[128,2048]{1,0:T(8,128)(2,1)S(1)} %copy-done.1, s32[1024]{0:T(1024)S(1)} %fusion.83), kind=kCustom, calls=%fused_computation | custom fusion | bytes 8392704 | tf_op jit(solution)/shard_map/gather | solution.py:90
  22.2 2.5 broadcast_select_fusion
  24.7 1.8 fusion.91
  26.5 68.2 %all_to_all.25 = bf16[64,8,2048]{2,1,0:T(8,128)(2,1)} all-to-all(bf16[64,8,2048]{2,1,0:T(8,128)(2,1)S(1)} %get-tuple-element.6), channel_id=1, replica_groups=mesh['wide'=64,'narrow'=4] {'wide'}, dimensions={0} | all-to-all | bytes 4194304 | tf_op jit(solution)/shard_map/all_to_all | solution.py:20
  94.7 10.2 %all-to-all-start.1 = ((bf16[64,8,2048]{2,1,0:T(8,128)(2,1)}), bf16[64,8,2048]{2,1,0:T(8,128)(2,1)}, u32[]{:S(2)}, u32[]{:S(2)}) async-start(bf16[64,8,2048]{2,1,0:T(8,128)(2,1)} %get-tuple-element.5), calls=%async_computation.1 | async-start | bytes 4194304 | tf_op jit(solution)/shard_map/all_to_all | solution.py:20
  105.7 3.4 %fusion.6 = f32[512,352]{0,1:T(8,128)} fusion(bf16[64,8,2048]{2,1,0:T(8,128)(2,1)} %all_to_all.25, bf16[1,2048,352]{1,2,0:T(8,128)(2,1)S(1)} %copy-done.3), kind=kOutput, calls=%fused_computation.15 | convolution fusion | flops 738197504 | bytes 4259840 | tf_op jit(solution)/shard_map/dot_general | solution.py:52
  109.1 5.7 %convolution_convert_fusion = bf16[512,2048]{1,0:T(8,128)(2,1)} fusion(bf16[1,352,2048]{2,1,0:T(8,128)(2,1)S(1)} %copy-done, bf16[1,2048,352]{1,2,0:T(8,128)(2,1)} %param.16, bf16[64,8,2048]{2,1,0:T(8,128)(2,1)} %all_to_all.25, f32[512,352]{0,1:T(8,128)} %fusion.6), kind=kOutput, calls=%fused_computation.10 | convolution fusion | flops 1478524928 | bytes 7798784 | tf_op jit(solution)/shard_map/dot_general | solution.py:55
  114.8 46.5 %all-to-all-done.1 = bf16[64,8,2048]{2,1,0:T(8,128)(2,1)} async-done(((bf16[64,8,2048]{2,1,0:T(8,128)(2,1)}), bf16[64,8,2048]{2,1,0:T(8,128)(2,1)}, u32[]{:S(2)}, u32[]{:S(2)}) %all-to-all-start.1) | async-done | bytes 2097184 | tf_op jit(solution)/shard_map/all_to_all | solution.py:20
  161.3 3.4 %fusion.10 = f32[512,352]{0,1:T(8,128)} fusion(bf16[64,8,2048]{2,1,0:T(8,128)(2,1)} %all-to-all-done.1, bf16[1,2048,352]{1,2,0:T(8,128)(2,1)S(1)} %copy-done.3), kind=kOutput, calls=%fused_computation.19 | convolution fusion | flops 738197504 | bytes 4259840 | tf_op jit(solution)/shard_map/dot_general | solution.py:52
  164.7 5.8 %convolution_convert_fusion.1 = bf16[512,2048]{1,0:T(8,128)(2,1)} fusion(bf16[1,352,2048]{2,1,0:T(8,128)(2,1)S(1)} %copy-done, bf16[1,2048,352]{1,2,0:T(8,128)(2,1)} %param.16, bf16[64,8,2048]{2,1,0:T(8,128)(2,1)} %all-to-all-done.1, f32[512,352]{0,1:T(8,128)} %fusion.10), kind=kOutput, calls=%fused_computation.11 | convolution fusion | flops 1478524928 | bytes 7798784 | tf_op jit(solution)/shard_map/dot_general | solution.py:55
  170.5 2.5 copy_bitcast_fusion
  173.0 59.4 %all_to_all.26 = bf16[4,64,16,512]{3,2,1,0:T(8,128)(2,1)} all-to-all(bf16[4,64,16,512]{3,2,1,0:T(8,128)(2,1)S(1)} %copy_bitcast_fusion), channel_id=1, replica_groups=mesh['wide'=64,'narrow'=4] {'narrow'}, dimensions={0} | all-to-all | bytes 8388608 | tf_op jit(solution)/shard_map/all_to_all | solution.py:36
  232.4 4.4 %reduce_sum.44 = bf16[64,16,512]{2,1,0:T(8,128)(2,1)} reduce(bf16[4,64,16,512]{3,2,1,0:T(8,128)(2,1)} %all_to_all.26, bf16[]{:T(256)} %constant.35.clone.1), dimensions={0}, to_apply=%region_5.6 | reduce | flops 1572864 | bytes 5242882 | tf_op jit(solution)/shard_map/reduce_sum | solution.py:37
  236.9 9.4 %all-to-all-start.4 = ((bf16[64,16,512]{2,1,0:T(8,128)(2,1)}), bf16[64,16,512]{2,1,0:T(8,128)(2,1)S(1)}, u32[]{:S(2)}, u32[]{:S(2)}) async-start(bf16[64,16,512]{2,1,0:T(8,128)(2,1)} %reduce_sum.44), calls=%async_computation.4 | async-start | bytes 2097152 | tf_op jit(solution)/shard_map/all_to_all | solution.py:98
  246.3 3.6 %fusion.38 = f32[128,704]{0,1:T(8,128)} fusion(bf16[128,2048]{1,0:T(8,128)(2,1)S(1)} %copy-done.1, bf16[2048,1408]{1,0:T(8,128)(2,1)} %all-gather.3.cloned.1.call-done), kind=kOutput, calls=%fused_computation.32 | convolution fusion | flops 369098752 | bytes 4030464 | tf_op jit(solution)/shard_map/dot_general | solution.py:104
  250.0 50.0 %all-gather.5.cloned.1.call-done = bf16[704,2048]{0,1:T(8,128)(2,1)} async-done(((bf16[704,32]{0,1:T(8,128)(2,1)}), bf16[704,2048]{0,1:T(8,128)(2,1)}) %all-gather.5.cloned.1.call-update) | async-done | bytes 2883600 | tf_op jit(solution)/shard_map/all_gather | solution.py:109
  299.9 7.4 %convolution_convert_fusion.2 = bf16[128,2048]{1,0:T(8,128)(2,1)S(1)} fusion(bf16[704,2048]{0,1:T(8,128)(2,1)} %all-gather.5.cloned.1.call-done, bf16[128,2048]{1,0:T(8,128)(2,1)S(1)} %copy-done.1, bf16[2048,1408]{1,0:T(8,128)(2,1)} %all-gather.3.cloned.1.call-done, f32[128,704]{0,1:T(8,128)} %fusion.38), kind=kOutput, calls=%fused_computation.12 | convolution fusion | flops 739000320 | bytes 7700480 | tf_op jit(solution)/shard_map/dot_general | solution.py:107
  308.2 8.4 %all-to-all-start = ((bf16[4,128,512]{2,1,0:T(8,128)(2,1)}), bf16[4,128,512]{2,1,0:T(8,128)(2,1)}, u32[]{:S(2)}, u32[]{:S(2)}) async-start(bf16[4,128,512]{2,1,0:T(8,128)(2,1)} %bitcast.93), calls=%async_computation | async-start | bytes 1048576 | tf_op jit(solution)/shard_map/all_to_all | solution.py:36
  317.3 3.3 gather_fusion.1
  321.9 2.2 multiply_reduce_fusion
  325.7 1.6 add_convert_fusion
  (35 shorter events, 7.8 us)
Async XLA Ops:
  6.5 102.6 %copy-start = (bf16[1,352,2048]{2,1,0:T(8,128)(2,1)S(1)}, bf16[1,352,2048]{2,1,0:T(8,128)(2,1)}, u32[]{:S(2)}) copy-start(bf16[1,352,2048]{2,1,0:T(8,128)(2,1)} %param.17) | copy-start | bytes 4325380
  6.5 9.6 %copy-start.1 = (bf16[128,2048]{1,0:T(8,128)(2,1)S(1)}, bf16[128,2048]{1,0:T(8,128)(2,1)}, u32[]{:S(2)}) copy-start(bf16[128,2048]{1,0:T(8,128)(2,1)} %param.9) | copy-start | bytes 1572868
  6.5 239.8 %all-gather.3.cloned.1.call-start = ((), (), s32[]{:S(2)}) async-start(), calls=%async_computation.5 | async-start | bytes 5857280 | tf_op jit(solution)/shard_map/all_gather | solution.py:46
  94.7 11.0 %copy-start.3 = (bf16[1,2048,352]{1,2,0:T(8,128)(2,1)S(1)}, bf16[1,2048,352]{1,2,0:T(8,128)(2,1)}, u32[]{:S(2)}) copy-start(bf16[1,2048,352]{1,2,0:T(8,128)(2,1)} %param.15) | copy-start | bytes 4325380
  94.7 66.6 %all-to-all-start.1 = ((bf16[64,8,2048]{2,1,0:T(8,128)(2,1)}), bf16[64,8,2048]{2,1,0:T(8,128)(2,1)}, u32[]{:S(2)}, u32[]{:S(2)}) async-start(bf16[64,8,2048]{2,1,0:T(8,128)(2,1)} %get-tuple-element.5), calls=%async_computation.1 | async-start | bytes 4194304 | tf_op jit(solution)/shard_map/all_to_all | solution.py:20
  104.9 195.0 %all-gather.5.cloned.1.call-start = ((), (), s32[]{:S(2)}) async-start(), calls=%async_computation.6 | async-start | bytes 3194880 | tf_op jit(solution)/shard_map/all_gather | solution.py:109
  236.9 71.3 %all-to-all-start.4 = ((bf16[64,16,512]{2,1,0:T(8,128)(2,1)}), bf16[64,16,512]{2,1,0:T(8,128)(2,1)S(1)}, u32[]{:S(2)}, u32[]{:S(2)}) async-start(bf16[64,16,512]{2,1,0:T(8,128)(2,1)} %reduce_sum.44), calls=%async_computation.4 | async-start | bytes 2097152 | tf_op jit(solution)/shard_map/all_to_all | solution.py:98
  307.3 9.2 %copy-start.2 = (f32[128,6]{0,1:T(8,128)S(1)}, f32[128,6]{0,1:T(8,128)}, u32[]{:S(2)}) copy-start(f32[128,6]{0,1:T(8,128)} %param.11) | copy-start | bytes 9220
  308.2 16.3 %all-to-all-start = ((bf16[4,128,512]{2,1,0:T(8,128)(2,1)}), bf16[4,128,512]{2,1,0:T(8,128)(2,1)}, u32[]{:S(2)}, u32[]{:S(2)}) async-start(bf16[4,128,512]{2,1,0:T(8,128)(2,1)} %bitcast.93), calls=%async_computation | async-start | bytes 1048576 | tf_op jit(solution)/shard_map/all_to_all | solution.py:36
Sparse Core Ops, SparseCore 0:
  10.8 162.8 all-gather.2
  177.4 122.4 all-gather.4
where the time goes:
time: 335 us; the launch traced here: 334 us
  blocking collectives  128 us (38%)
  waiting for transfers between devices  97.5 us (29%)
  matrix products  29.3 us (9%)
  starting transfers between devices  28.1 us (8%)
  local copies, waits for them, and re-layouts  19.1 us (6%)
  other arithmetic  18.9 us (6%)
  between operations  13.6 us (4%)
    all_to_all x1, blocking collectives, items_in_groups(): lax.all_to_all(group, axis, split_axis=split_dim, concat_axis=concat_dim,...  68.2 us
    all_to_all x1, blocking collectives, sum_at_owner(): lax.all_to_all(split_up(array, dim, length), axis, 0, 0, tiled=True)  59.4 us
    all_gather x1, waiting for transfers between devices, body(): lax.all_gather(shared_down, 'wide', axis=1, tiled=True)  50 us
    all_to_all x1, waiting for transfers between devices, items_in_groups(): lax.all_to_all(group, axis, split_axis=split_dim, concat_axis=concat_dim,...  46.5 us
    dot_general x2, matrix products, expert_ffn(): jnp.dot(hidden, w_down, preferred_element_type=jnp.float32)  11.5 us
    all_to_all x1, starting transfers between devices, items_in_groups(): lax.all_to_all(group, axis, split_axis=split_dim, concat_axis=concat_dim,...  10.2 us
    all_to_all x1, starting transfers between devices, body(): lax.all_to_all(expert_out, 'wide', split_axis=0, concat_axis=0, tiled=True)  9.44 us
    all_to_all x1, starting transfers between devices, sum_at_owner(): lax.all_to_all(split_up(array, dim, length), axis, 0, 0, tiled=True)  8.38 us
  transfers between devices with their start and end apart: 5, of which 3 were waited for; matrix products, arithmetic and copies ran while one was open for 19% of the time, Pallas kernels for 0%

commit v1 on v0

--- a/solution.py
+++ b/solution.py
@@ -106,7 +106,9 @@
     shared_hidden = (jax.nn.silu(gate_sum) * up_sum).astype(jnp.bfloat16)
     shared_terms = jnp.dot(
         shared_hidden,
-        lax.all_gather(shared_down, "wide", axis=1, tiled=True),
+        jnp.concatenate(
+            lax.all_to_all(jnp.stack([shared_down] * lax.axis_size("wide")), "wide", 0, 0), axis=1
+        ),
         preferred_element_type=jnp.float32,
     )
     shared = sum_at_owner(shared_terms.astype(jnp.bfloat16), "narrow", 1)

time: 335 us -> 387 us (1.16)
  waiting for transfers between devices: 97.5 us -> 133 us
  blocking collectives: 128 us -> 141 us
    all_to_all x0 -> x1, waiting for transfers between devices: none -> 72.5 us  [body(): lax.all_to_all(jnp.stack([shared_down] * lax.axis_size('wide')), 'wide',...]
    all_gather x1 -> x0, waiting for transfers between devices: 50 us -> none  [body(): lax.all_gather(shared_down, 'wide', axis=1, tiled=True)]
    all_to_all x1, blocking collectives: 59.4 us -> 76.9 us  [sum_at_owner(): lax.all_to_all(split_up(array, dim, length), axis, 0, 0, tiled=True)]
    all_to_all x1, waiting for transfers between devices: 0.01 us -> 14.9 us  [body(): lax.all_to_all(expert_out, 'wide', split_axis=0, concat_axis=0, tiled=True)]
    all_to_all x0 -> x1, starting transfers between devices: none -> 6.18 us  [body(): lax.all_to_all(jnp.stack([shared_down] * lax.axis_size('wide')), 'wide',...]
    all_to_all x1, blocking collectives: 68.2 us -> 64 us  [items_in_groups(): lax.all_to_all(group, axis, split_axis=split_dim, concat_axis=concat_dim,...]
  transfers between devices with their start and end apart: 5 -> 5, of which waited for: 3 -> 3; matrix products, arithmetic and copies ran while one was open for 19% -> 12% of each run, Pallas kernels for 0% -> 0%
where the time goes in v1:
time: 387 us; the launch traced here: 386 us
  blocking collectives  141 us (36%)
  waiting for transfers between devices  133 us (34%)
  starting transfers between devices  31.5 us (8%)
  matrix products  29 us (7%)
  local copies, waits for them, and re-layouts  21.6 us (6%)
  other arithmetic  16.2 us (4%)
  between operations  13.6 us (4%)
    all_to_all x1, blocking collectives, sum_at_owner(): lax.all_to_all(split_up(array, dim, length), axis, 0, 0, tiled=True)  76.9 us
    all_to_all x1, waiting for transfers between devices, body(): lax.all_to_all(jnp.stack([shared_down] * lax.axis_size('wide')), 'wide',...  72.5 us
    all_to_all x1, blocking collectives, items_in_groups(): lax.all_to_all(group, axis, split_axis=split_dim, concat_axis=concat_dim,...  64 us
    all_to_all x1, waiting for transfers between devices, items_in_groups(): lax.all_to_all(group, axis, split_axis=split_dim, concat_axis=concat_dim,...  45.9 us
    all_to_all x1, waiting for transfers between devices, body(): lax.all_to_all(expert_out, 'wide', split_axis=0, concat_axis=0, tiled=True)  14.9 us
    dot_general x2, matrix products, expert_ffn(): jnp.dot(hidden, w_down, preferred_element_type=jnp.float32)  11.1 us
    all_to_all x1, starting transfers between devices, items_in_groups(): lax.all_to_all(group, axis, split_axis=split_dim, concat_axis=concat_dim,...  9.59 us
    all_to_all x1, starting transfers between devices, sum_at_owner(): lax.all_to_all(split_up(array, dim, length), axis, 0, 0, tiled=True)  8.03 us
  transfers between devices with their start and end apart: 5, of which 3 were waited for; matrix products, arithmetic and copies ran while one was open for 12% of the time, Pallas kernels for 0%

profile of v1, /device:TPU:1, one launch (start us, length us, event | category | flops | bytes accessed | tf_op | source)
XLA Modules:
  0.0 386.3 jit_solution(1035290873174867259)
XLA Ops:
  11.0 3.4 scatter_custom_fusion
  14.5 6.0 %gather_fusion = bf16[1024,2048]{1,0:T(8,128)(2,1)} fusion(bf16[128,2048]{1,0:T(8,128)(2,1)S(1)} %copy-done.1, s32[1024]{0:T(1024)S(1)} %fusion.83), kind=kCustom, calls=%fused_computation | custom fusion | bytes 8392704 | tf_op jit(solution)/shard_map/gather | solution.py:90
  20.5 2.5 broadcast_select_fusion
  24.8 64.0 %all_to_all.30 = bf16[64,8,2048]{2,1,0:T(8,128)(2,1)} all-to-all(bf16[64,8,2048]{2,1,0:T(8,128)(2,1)S(1)} %get-tuple-element.6), channel_id=1, replica_groups=mesh['wide'=64,'narrow'=4] {'wide'}, dimensions={0} | all-to-all | bytes 4194304 | tf_op jit(solution)/shard_map/all_to_all | solution.py:20
  88.8 9.6 %all-to-all-start.2 = ((bf16[64,8,2048]{2,1,0:T(8,128)(2,1)}), bf16[64,8,2048]{2,1,0:T(8,128)(2,1)}, u32[]{:S(2)}, u32[]{:S(2)}) async-start(bf16[64,8,2048]{2,1,0:T(8,128)(2,1)} %get-tuple-element.5), calls=%async_computation.2 | async-start | bytes 4194304 | tf_op jit(solution)/shard_map/all_to_all | solution.py:20
  99.2 3.5 fusion.6
  102.7 45.9 %all-to-all-done.2 = bf16[64,8,2048]{2,1,0:T(8,128)(2,1)} async-done(((bf16[64,8,2048]{2,1,0:T(8,128)(2,1)}), bf16[64,8,2048]{2,1,0:T(8,128)(2,1)}, u32[]{:S(2)}, u32[]{:S(2)}) %all-to-all-start.2) | async-done | bytes 2097184 | tf_op jit(solution)/shard_map/all_to_all | solution.py:20
  148.5 3.4 fusion.10
  151.9 5.8 %convolution_convert_fusion = bf16[512,2048]{1,0:T(8,128)(2,1)} fusion(bf16[1,352,2048]{2,1,0:T(8,128)(2,1)S(1)} %copy-done, bf16[1,2048,352]{1,2,0:T(8,128)(2,1)} %param.16, bf16[64,8,2048]{2,1,0:T(8,128)(2,1)} %all_to_all.30, f32[512,352]{0,1:T(8,128)} %fusion.6), kind=kOutput, calls=%fused_computation.10 | convolution fusion | flops 1478524928 | bytes 7798784 | tf_op jit(solution)/shard_map/dot_general | solution.py:55
  157.7 5.3 %convolution_convert_fusion.1 = bf16[512,2048]{1,0:T(8,128)(2,1)} fusion(bf16[1,352,2048]{2,1,0:T(8,128)(2,1)S(1)} %copy-done, bf16[1,2048,352]{1,2,0:T(8,128)(2,1)S(1)} %copy-done.7, bf16[64,8,2048]{2,1,0:T(8,128)(2,1)} %all-to-all-done.2, f32[512,352]{0,1:T(8,128)} %fusion.10), kind=kOutput, calls=%fused_computation.11 | convolution fusion | flops 1478524928 | bytes 7798784 | tf_op jit(solution)/shard_map/dot_general | solution.py:55
  163.1 2.5 copy_bitcast_fusion
  165.6 76.9 %all_to_all.31 = bf16[4,64,16,512]{3,2,1,0:T(8,128)(2,1)} all-to-all(bf16[4,64,16,512]{3,2,1,0:T(8,128)(2,1)S(1)} %copy_bitcast_fusion), channel_id=1, replica_groups=mesh['wide'=64,'narrow'=4] {'narrow'}, dimensions={0} | all-to-all | bytes 8388608 | tf_op jit(solution)/shard_map/all_to_all | solution.py:36
  242.6 2.0 stack.2
  244.6 6.2 %all-to-all-start = ((bf16[64,704,32]{1,2,0:T(8,128)(2,1)}), bf16[64,704,32]{1,2,0:T(8,128)(2,1)}, u32[]{:S(2)}, u32[]{:S(2)}) async-start(bf16[64,704,32]{1,2,0:T(8,128)(2,1)} %stack.2), calls=%async_computation | async-start | bytes 6291456 | tf_op jit(solution)/shard_map/all_to_all | solution.py:110
  250.8 4.4 %reduce_sum.44 = bf16[64,16,512]{2,1,0:T(8,128)(2,1)} reduce(bf16[4,64,16,512]{3,2,1,0:T(8,128)(2,1)} %all_to_all.31, bf16[]{:T(256)} %constant.35.clone.1), dimensions={0}, to_apply=%region_5.6 | reduce | flops 1572864 | bytes 5242882 | tf_op jit(solution)/shard_map/reduce_sum | solution.py:37
  255.2 72.5 %all-to-all-done = bf16[64,704,32]{1,2,0:T(8,128)(2,1)} async-done(((bf16[64,704,32]{1,2,0:T(8,128)(2,1)}), bf16[64,704,32]{1,2,0:T(8,128)(2,1)}, u32[]{:S(2)}, u32[]{:S(2)}) %all-to-all-start) | async-done | bytes 2883616 | tf_op jit(solution)/shard_map/all_to_all | solution.py:110
  327.7 7.7 %all-to-all-start.5 = ((bf16[64,16,512]{2,1,0:T(8,128)(2,1)}), bf16[64,16,512]{2,1,0:T(8,128)(2,1)S(1)}, u32[]{:S(2)}, u32[]{:S(2)}) async-start(bf16[64,16,512]{2,1,0:T(8,128)(2,1)} %reduce_sum.44), calls=%async_computation.5 | async-start | bytes 2097152 | tf_op jit(solution)/shard_map/all_to_all | solution.py:98
  335.5 3.7 fusion.38
  339.1 7.4 %convolution_convert_fusion.2 = bf16[128,2048]{1,0:T(8,128)(2,1)S(1)} fusion(bf16[704,2048]{0,1:T(8,128)(2,1)} %bitcast.3, bf16[128,2048]{1,0:T(8,128)(2,1)S(1)} %copy-done.1, bf16[2048,1408]{1,0:T(8,128)(2,1)} %all-gather.2.cloned.1.call-done, f32[128,704]{0,1:T(8,128)} %fusion.38), kind=kOutput, calls=%fused_computation.12 | convolution fusion | flops 739000320 | bytes 7700480 | tf_op jit(solution)/shard_map/dot_general | solution.py:107
  347.4 14.9 %all-to-all-done.5 = bf16[64,16,512]{2,1,0:T(8,128)(2,1)S(1)} async-done(((bf16[64,16,512]{2,1,0:T(8,128)(2,1)}), bf16[64,16,512]{2,1,0:T(8,128)(2,1)S(1)}, u32[]{:S(2)}, u32[]{:S(2)}) %all-to-all-start.5) | async-done | bytes 1048608 | tf_op jit(solution)/shard_map/all_to_all | solution.py:98
  362.3 8.0 %all-to-all-start.1 = ((bf16[4,128,512]{2,1,0:T(8,128)(2,1)}), bf16[4,128,512]{2,1,0:T(8,128)(2,1)S(1)}, u32[]{:S(2)}, u32[]{:S(2)}) async-start(bf16[4,128,512]{2,1,0:T(8,128)(2,1)} %bitcast.96), calls=%async_computation.1 | async-start | bytes 1048576 | tf_op jit(solution)/shard_map/all_to_all | solution.py:36
  370.5 3.3 gather_fusion.1
  373.8 2.5 reshape.99
  376.3 2.3 multiply_reduce_fusion
  (43 shorter events, 8.8 us)
Async XLA Ops:
  6.5 145.4 %copy-start = (bf16[1,352,2048]{2,1,0:T(8,128)(2,1)S(1)}, bf16[1,352,2048]{2,1,0:T(8,128)(2,1)}, u32[]{:S(2)}) copy-start(bf16[1,352,2048]{2,1,0:T(8,128)(2,1)} %param.17) | copy-start | bytes 4325380
  6.5 8.0 %copy-start.1 = (bf16[128,2048]{1,0:T(8,128)(2,1)S(1)}, bf16[128,2048]{1,0:T(8,128)(2,1)}, u32[]{:S(2)}) copy-start(bf16[128,2048]{1,0:T(8,128)(2,1)} %param.9) | copy-start | bytes 1572868
  88.8 9.7 %copy-start.2 = (bf16[32,704]{1,0:T(8,128)(2,1)S(1)}, bf16[32,704]{1,0:T(8,128)(2,1)}, u32[]{:S(2)}) copy-start(bf16[32,704]{1,0:T(8,128)(2,1)} %param.13) | copy-start | bytes 135172
  88.8 9.7 %copy-start.3 = (bf16[32,704]{1,0:T(8,128)(2,1)S(1)}, bf16[32,704]{1,0:T(8,128)(2,1)}, u32[]{:S(2)}) copy-start(bf16[32,704]{1,0:T(8,128)(2,1)} %param.12) | copy-start | bytes 135172
  88.8 10.4 %copy-start.6 = (bf16[1,2048,352]{1,2,0:T(8,128)(2,1)S(1)}, bf16[1,2048,352]{1,2,0:T(8,128)(2,1)}, u32[]{:S(2)}) copy-start(bf16[1,2048,352]{1,2,0:T(8,128)(2,1)} %param.15) | copy-start | bytes 4325380
  88.8 59.7 %all-to-all-start.2 = ((bf16[64,8,2048]{2,1,0:T(8,128)(2,1)}), bf16[64,8,2048]{2,1,0:T(8,128)(2,1)}, u32[]{:S(2)}, u32[]{:S(2)}) async-start(bf16[64,8,2048]{2,1,0:T(8,128)(2,1)} %get-tuple-element.5), calls=%async_computation.2 | async-start | bytes 4194304 | tf_op jit(solution)/shard_map/all_to_all | solution.py:20
  98.4 237.1 %all-gather.2.cloned.1.call-start = ((), (), s32[]{:S(2)}) async-start(), calls=%async_computation.6 | async-start | bytes 5857280 | tf_op jit(solution)/shard_map/all_gather | solution.py:46
  151.9 5.8 %copy-start.7 = (bf16[1,2048,352]{1,2,0:T(8,128)(2,1)S(1)}, bf16[1,2048,352]{1,2,0:T(8,128)(2,1)}, u32[]{:S(2)}) copy-start(bf16[1,2048,352]{1,2,0:T(8,128)(2,1)} %param.16) | copy-start | bytes 4325380
  165.6 77.0 %copy-start.4 = (bf16[704,32]{0,1:T(8,128)(2,1)S(1)}, bf16[704,32]{0,1:T(8,128)(2,1)}, u32[]{:S(2)}) copy-start(bf16[704,32]{0,1:T(8,128)(2,1)} %param.14) | copy-start | bytes 135172
  244.6 83.1 %all-to-all-start = ((bf16[64,704,32]{1,2,0:T(8,128)(2,1)}), bf16[64,704,32]{1,2,0:T(8,128)(2,1)}, u32[]{:S(2)}, u32[]{:S(2)}) async-start(bf16[64,704,32]{1,2,0:T(8,128)(2,1)} %stack.2), calls=%async_computation | async-start | bytes 6291456 | tf_op jit(solution)/shard_map/all_to_all | solution.py:110
  327.7 34.6 %all-to-all-start.5 = ((bf16[64,16,512]{2,1,0:T(8,128)(2,1)}), bf16[64,16,512]{2,1,0:T(8,128)(2,1)S(1)}, u32[]{:S(2)}, u32[]{:S(2)}) async-start(bf16[64,16,512]{2,1,0:T(8,128)(2,1)} %reduce_sum.44), calls=%async_computation.5 | async-start | bytes 2097152 | tf_op jit(solution)/shard_map/all_to_all | solution.py:98
  346.5 23.8 %copy-start.5 = (f32[128,6]{0,1:T(8,128)S(1)}, f32[128,6]{0,1:T(8,128)}, u32[]{:S(2)}) copy-start(f32[128,6]{0,1:T(8,128)} %param.11) | copy-start | bytes 9220
  362.3 16.3 %all-to-all-start.1 = ((bf16[4,128,512]{2,1,0:T(8,128)(2,1)}), bf16[4,128,512]{2,1,0:T(8,128)(2,1)S(1)}, u32[]{:S(2)}, u32[]{:S(2)}) async-start(bf16[4,128,512]{2,1,0:T(8,128)(2,1)} %bitcast.96), calls=%async_computation.1 | async-start | bytes 1048576 | tf_op jit(solution)/shard_map/all_to_all | solution.py:36
Sparse Core Ops, SparseCore 0:
  102.7 163.3 all-gather.1
